TPU v7x, 256 devices: a whole 4x4x8 slice. The times are simulated.
256 devices in a mesh: feat: 8 (over y, core), rows: 32 (over z, x).
Axes of the slice: x: 4, y: 4, z: 8, core: 2. Of those that a mesh axis runs over, the one named last changes fastest.
Arguments:
- bin_index: int32 [128, 262144], P('feat', 'rows'), may hold values from 0 to 255
- node_ids: int32 [262144], P('rows'), may hold values from 0 to 31
- gradients: int32 [262144], P('rows'), may hold values from -32 to 32
- hessians: int32 [262144], P('rows'), may hold values from 1 to 32
Outputs:
- split_gains: float32 [32, 128, 256], P('rows', 'feat')
- best_gains: float32 [32], P('rows')
All inputs are finite; a program needn't handle non-finite values.
Results may differ from a plain program's by a relative error of at most 0.0003.
Values sent between devices are 32-bit elements; how exact they have to be, the bound alone decides.
A program may use at most 64 MiB of HBM per device.

v0:
```python
import jax
import jax.numpy as jnp
from jax import lax
from jax.sharding import PartitionSpec as P

BINS = 256
NODE_DEV = 1


shrinkage = 1.0


def in_blocks(shard, dim, devices):
    before, after = (shard.shape[:dim], shard.shape[dim + 1 :])
    return jnp.moveaxis(shard.reshape(*before, devices, -1, *after), dim, 0)


def sum_at_owner(shard, axis, dim):
    tiles = in_blocks(shard, dim, lax.axis_size(axis))
    arrived = lax.all_to_all(tiles, axis, split_axis=0, concat_axis=0, tiled=True)
    return arrived.sum(axis=0)


def sent_to_all(shard, axis):
    copies = jnp.broadcast_to(shard, (lax.axis_size(axis), *shard.shape))
    return lax.all_to_all(copies, axis, split_axis=0, concat_axis=0, tiled=True)


def of_everyone(shard, axis):
    everything = sent_to_all(shard, axis)
    return jnp.max(everything, axis=0)


def gains_of(grad_hist, hess_hist):
    left_grad = jnp.cumsum(grad_hist, axis=-1)
    left_hess = jnp.cumsum(hess_hist, axis=-1)
    total_grad = left_grad[..., -1:]
    total_hess = left_hess[..., -1:]
    right_grad = total_grad - left_grad
    right_hess = total_hess - left_hess
    return 0.5 * (
        left_grad * left_grad / (left_hess + shrinkage)
        + right_grad * right_grad / (right_hess + shrinkage)
        - total_grad * total_grad / (total_hess + shrinkage)
    )


def per_device(bin_index, node_ids, gradients, hessians):
    feature_count, rows_here = bin_index.shape
    row_block = min(4096, rows_here)
    block_count = rows_here // row_block
    paired = jnp.stack([gradients, hessians], axis=1).astype(jnp.float32)
    bin_values = jnp.arange(BINS, dtype=jnp.int32)
    every_node = NODE_DEV * lax.axis_size("rows")
    node_values = jnp.arange(every_node, dtype=jnp.int32)

    def accumulate(running, block_number):
        offset = block_number * row_block
        bins_here = lax.dynamic_slice_in_dim(bin_index, offset, row_block, 1)
        nodes_here = lax.dynamic_slice_in_dim(node_ids, offset, row_block, 0)
        values_here = lax.dynamic_slice_in_dim(paired, offset, row_block, 0)
        node_hot = (nodes_here[:, None] - 0 == node_values[None, :]).astype(jnp.float32)
        weighted = (
            (node_hot[:, :, None] * values_here[:, None, :])
            .astype(jnp.bfloat16)
            .reshape(row_block, every_node * 2)
        )
        updated = []
        for feature_index in range(feature_count):
            bin_hot = (bins_here[feature_index][:, None] == bin_values[None, :]).astype(
                jnp.bfloat16
            )
            product = lax.dot_general(
                weighted, bin_hot, (((0,), (0,)), ((), ())), preferred_element_type=jnp.float32
            )
            updated.append(running[feature_index] + product)
        return (tuple(updated), None)

    start_sums = tuple(
        (jnp.zeros((every_node * 2, BINS), jnp.float32) for feature_index in range(feature_count))
    )
    summed, unused = lax.scan(accumulate, start_sums, jnp.arange(block_count, dtype=jnp.int32))
    joined = jnp.stack(summed, axis=1)
    whole_table = joined.reshape(every_node, 2, feature_count, BINS)
    owned = sum_at_owner(whole_table, "rows", 0)
    split_gains = gains_of(owned[:, 0], owned[:, 1])
    local_best = jnp.max(split_gains, axis=(1, 2))
    best_gains = of_everyone(local_best, "feat")
    return (split_gains, best_gains)


def solution(mesh):
    in_specs = (P("feat", "rows"), P("rows"), P("rows"), P("rows"))
    out_specs = (P("rows", "feat", None), P("rows"))
    return jax.shard_map(
        per_device, mesh=mesh, in_specs=in_specs, out_specs=out_specs, check_vma=False
    )
```

profile of v0, /device:TPU:1, one launch (start us, length us, event | category | flops | bytes accessed | tf_op | source)
XLA Modules:
  0.0 99.0 jit_solution(13168714460628934398)
XLA Ops:
  1.6 41.3 %while.42 = (s32[]{:T(128)}, f32[64,256]{1,0:T(8,128)S(1)}, f32[64,256]{1,0:T(8,128)S(1)}, f32[64,256]{1,0:T(8,128)S(1)}, f32[64,256]{1,0:T(8,128)S(1)}, /*index...) while((s32[]{:T(128)}, f32[64,256]{1,0:T(8,128)S(1)}, ...), condition=%wide.region_1.2_spmd.clone.clone, body=%wide.region_0.1_spmd.clone.clone.sunk | while | flops 2165571584 | bytes 14041772 | solution.py:82
  3.6 2.6 %fusion.124 = (s32[1,4096]{1,0:T(1,128)S(1)}, s32[1,4096]{1,0:T(1,128)S(1)}, s32[1,4096]{1,0:T(1,128)S(1)}, s32[1,4096]{1,0:T(1,128)S(1)}, s32[1,4096]{1,0:T(1,1...) fusion(s32[16,8192]{1,0:T(8,128)} %get-tuple-element.661, ...), kind=kLoop, calls=%fused_computation.98.clone.1 | loop fusion | bytes 524352 | tf_op jit(solution)/shard_map/while/body/eval_jaxpr/slice | solution.py:70
  7.0 0.9 fusion.140
  8.0 0.9 fusion.139
  8.9 0.9 fusion.138
  11.7 0.9 fusion.135
  12.6 0.9 fusion.134
  13.6 0.9 fusion.133
  15.4 0.9 fusion.131
  16.4 0.9 fusion.130
  17.3 0.9 fusion.129
  20.1 0.9 fusion.126
  21.1 0.9 fusion.125
  24.0 2.9 %fusion.124 = (s32[1,4096]{1,0:T(1,128)S(1)}, s32[1,4096]{1,0:T(1,128)S(1)}, s32[1,4096]{1,0:T(1,128)S(1)}, s32[1,4096]{1,0:T(1,128)S(1)}, s32[1,4096]{1,0:T(1,1...) fusion(s32[16,8192]{1,0:T(8,128)} %get-tuple-element.661, ...), kind=kLoop, calls=%fused_computation.98.clone.1 | loop fusion | bytes 524352 | tf_op jit(solution)/shard_map/while/body/eval_jaxpr/slice | solution.py:70
  29.6 0.9 fusion.138
  30.5 0.9 fusion.137
  31.5 0.9 fusion.136
  33.4 0.9 fusion.134
  34.3 0.9 fusion.133
  35.2 0.9 fusion.132
  38.0 0.9 fusion.129
  41.8 0.9 fusion.125
  44.0 37.9 %all_to_all.11 = f32[32,1,2,16,256]{4,2,3,1,0:T(2,128)S(1)} all-to-all(f32[32,1,2,16,256]{4,2,3,1,0:T(2,128)S(1)} %constant_dynamic-update-slice_fusion), channel_id=1, replica_groups=mesh['feat'=8,'rows'=32] {'rows'}, dimensions={0} | all-to-all | bytes 2097152 | tf_op jit(solution)/shard_map/all_to_all | solution.py:20
  86.7 11.7 %all_to_all.12 = f32[8,1,1]{2,1,0:T(1,128)S(1)} all-to-all(f32[8,1,1]{2,1,0:T(1,128)S(1)} %broadcast_in_dim.2), channel_id=1, replica_groups=mesh['feat'=8,'rows'=32] {'feat'}, dimensions={0} | all-to-all | bytes 64 | tf_op jit(solution)/shard_map/all_to_all | solution.py:26
  (100 shorter events, 23.4 us)
where the time goes:
time: 99.4 us; the launch traced here: 99 us
  blocking collectives  49.5 us (50%)
  matrix products  29.7 us (30%)
  local copies, waits for them, and re-layouts  11.4 us (11%)
  other arithmetic  5.42 us (5%)
  loops' own time  1.82 us (2%)
  between operations  1.05 us (1%)
    all_to_all x1, blocking collectives, sum_at_owner(): lax.all_to_all(tiles, axis, split_axis=0, concat_axis=0, tiled=True)  37.9 us
    dot_general x32, matrix products, accumulate(): lax.dot_general(weighted, bin_hot, (((0,), (0,)), ((), ())), preferred_el...  29.7 us
    all_to_all x1, blocking collectives, sent_to_all(): return lax.all_to_all(copies, axis, split_axis=0, concat_axis=0, tiled=True)  11.7 us
    slice x2, local copies, waits for them, and re-layouts, accumulate(): bins_here[feature_index][:, None] == bin_values[None, :]  5.51 us

commit v1 on v0

v1 whole, which is shorter than its diff:
```python
import functools

import jax
import jax.numpy as jnp
from jax import lax
from jax.experimental import pallas as pl
from jax.experimental.pallas import tpu as pltpu
from jax.sharding import PartitionSpec as P

BINS = 256
HALF = 128
LANES = 128
BASE = 9
TOP = 8192
X = 4
Z = 8
FEAT = 8
GROUP = 4
BLOCK = 512
UNROLL = 16
shrinkage = 1.0
MESH = pl.DeviceIdType.MESH
f32 = jnp.float32
bf16 = jnp.bfloat16


def rows_of(row):
    return jnp.broadcast_to(row, (16, LANES)).astype(f32).astype(bf16)


def digit_rows(grad, hess):
    grad8 = jnp.broadcast_to(grad, (8, LANES))
    hess8 = jnp.broadcast_to(hess, (8, LANES))
    return jnp.concatenate([grad8, hess8], 0).astype(bf16)


def weights_of(node_ref, grad_ref, hess_ref, start, nodes_at):
    columns = []
    for tile in range(BLOCK // LANES):
        here = pl.ds(start + tile * LANES, LANES)
        node = rows_of(node_ref[0:1, here])
        grad = grad_ref[0:1, here].astype(f32)
        hess = hess_ref[0:1, here].astype(f32)
        grad_high = jnp.round(grad * (1.0 / BASE))
        hess_high = jnp.round(hess * (1.0 / BASE))
        low = digit_rows(grad - BASE * grad_high, hess - BASE * hess_high)
        high = digit_rows(grad_high, hess_high)
        none = jnp.zeros_like(low)
        masks = [node == nodes for nodes in nodes_at]
        column = [jnp.where(mask, low, none) for mask in masks]
        column += [jnp.where(mask, high, none) for mask in masks]
        columns.append(jnp.concatenate(column, 0))
    return jnp.concatenate(columns, 1)


def kernel(
    bins_ref,
    node_ref,
    grad_ref,
    hess_ref,
    out_ref,
    best_ref,
    weights,
    total,
    partial,
    x_in,
    z_out,
    z_in,
    best_out,
    best_in,
    x_send,
    x_recv,
    z_send,
    z_recv,
    b_send,
    b_recv,
):
    feature_count, row_count = bins_ref.shape
    groups = feature_count // GROUP
    feat = lax.axis_index("feat")
    rows = lax.axis_index("rows")
    my_z = rows // X
    my_x = rows % X

    x_peer = [my_z * X + (my_x + step) % X for step in range(X)]
    z_peer = [((my_z + step) % Z) * X + my_x for step in range(Z)]
    f_peer = [(feat + step) % FEAT for step in range(FEAT)]

    barrier = pltpu.get_barrier_semaphore()
    for step in range(1, X):
        pl.semaphore_signal(barrier, inc=1, device_id=(feat, x_peer[step]), device_id_type=MESH)
    for step in range(1, Z):
        pl.semaphore_signal(barrier, inc=1, device_id=(feat, z_peer[step]), device_id_type=MESH)
    for step in range(1, FEAT):
        pl.semaphore_signal(barrier, inc=1, device_id=(f_peer[step], rows), device_id_type=MESH)

    bin_at = lax.broadcasted_iota(jnp.int32, (HALF, LANES), 0).astype(f32).astype(bf16)
    nodes_at = [
        ((lax.broadcasted_iota(jnp.int32, (16, LANES), 0) % Z) * X + x).astype(f32).astype(bf16)
        for x in range(X)
    ]
    big = f32(1.5 * 2.0**36)

    def compute(group):
        def block(number, carry):
            start = pl.multiple_of(number * BLOCK, BLOCK)
            row_list = []
            for feature in range(GROUP):
                at = group * GROUP + feature
                columns = []
                for tile in range(BLOCK // LANES):
                    row = bins_ref[at : at + 1, pl.ds(start + tile * LANES, LANES)]
                    upper = row >= HALF
                    low = jnp.where(upper, row - HALF, row)
                    size = jnp.where(upper, TOP, 1)
                    low = jnp.concatenate([rows_of(low)] * (HALF // 16), 0)
                    size = jnp.concatenate([rows_of(size)] * (HALF // 16), 0)
                    columns.append(jnp.where(low <= bin_at, size, jnp.zeros_like(size)))
                row_list.append(jnp.concatenate(columns, 1))
            hot = jnp.concatenate(row_list, 0)
            if group == 0:
                weight = weights_of(node_ref, grad_ref, hess_ref, start, nodes_at)
                weights[:, pl.ds(start, BLOCK)] = weight
            else:
                weight = weights[:, pl.ds(start, BLOCK)]
            product = lax.dot_general(
                hot, weight, (((1,), (1,)), ((), ())), preferred_element_type=f32
            )
            upper_part = (product + big) - big
            total[0] += product - upper_part
            total[1] += upper_part
            return carry

        total[...] = jnp.zeros_like(total)
        lax.fori_loop(0, row_count // BLOCK, block, 0, unroll=UNROLL)
        for feature in range(GROUP):
            at = slice(feature * HALF, (feature + 1) * HALF)
            for half in range(2):
                turned = total[half, at, :].T
                joined = turned[: LANES // 2] + BASE * turned[LANES // 2 :]
                if half:
                    joined = joined * (1.0 / TOP)
                for x in range(X):
                    partial[group, x, feature, :, half * HALF : (half + 1) * HALF] = joined[
                        x * 16 : (x + 1) * 16
                    ]

    def x_copy(group, step):
        return pltpu.make_async_remote_copy(
            src_ref=partial.at[group, (my_x + step) % X],
            dst_ref=x_in.at[group, step - 1],
            send_sem=x_send.at[group, step - 1],
            recv_sem=x_recv.at[group, step - 1],
            device_id=(feat, x_peer[step]),
            device_id_type=MESH,
        )

    def z_copy(group, step):
        return pltpu.make_async_remote_copy(
            src_ref=z_out.at[group, (my_z + step) % Z],
            dst_ref=z_in.at[group, step - 1],
            send_sem=z_send.at[group, step - 1],
            recv_sem=z_recv.at[group, step - 1],
            device_id=(feat, z_peer[step]),
            device_id_type=MESH,
        )

    def best_copy(step):
        return pltpu.make_async_remote_copy(
            src_ref=best_out,
            dst_ref=best_in.at[step - 1],
            send_sem=b_send.at[step - 1],
            recv_sem=b_recv.at[step - 1],
            device_id=(f_peer[step], rows),
            device_id_type=MESH,
        )

    def start_x(group):
        for step in range(1, X):
            x_copy(group, step).start()

    def x_to_z(group):
        for step in range(1, X):
            x_copy(group, step).wait_recv()
        for feature in range(GROUP):
            summed = partial[group, my_x, feature]
            for step in range(1, X):
                summed = summed + x_in[group, step - 1, feature]
            for part in range(2):
                for z in range(Z):
                    z_out[group, z, part * GROUP + feature : part * GROUP + feature + 1, :] = summed[
                        part * Z + z : part * Z + z + 1
                    ]
        for step in range(1, Z):
            z_copy(group, step).start()

    def finish(group):
        for step in range(1, Z):
            z_copy(group, step).wait_recv()
        summed = z_out[group, my_z]
        for step in range(1, Z):
            summed = summed + z_in[group, step - 1]
        first = summed[:, :HALF]
        second = summed[:, HALF:] + first[:, HALF - 1 :]
        whole = second[:, HALF - 1 :]
        left = jnp.concatenate([first, second], 1)
        right = whole - left
        left_grad, left_hess = left[:GROUP], left[GROUP:]
        right_grad, right_hess = right[:GROUP], right[GROUP:]
        whole_grad, whole_hess = whole[:GROUP], whole[GROUP:]
        gains = 0.5 * (
            left_grad * left_grad / (left_hess + shrinkage)
            + right_grad * right_grad / (right_hess + shrinkage)
            - whole_grad * whole_grad / (whole_hess + shrinkage)
        )
        out_ref[0, group * GROUP : (group + 1) * GROUP, :] = gains

    for group in range(groups):
        compute(group)
        if group == 0:
            pl.semaphore_wait(barrier, X - 1 + Z - 1 + FEAT - 1)
        start_x(group)
        if group >= 1:
            x_to_z(group - 1)
        if group >= 2:
            finish(group - 2)
    x_to_z(groups - 1)
    finish(groups - 2)
    finish(groups - 1)
    gains = out_ref[0]
    top = jnp.max(jnp.max(gains, axis=1, keepdims=True), axis=0, keepdims=True)
    best_out[...] = jnp.broadcast_to(top, best_out.shape)
    for step in range(1, FEAT):
        best_copy(step).start()
    best = best_out[...]
    for step in range(1, FEAT):
        best_copy(step).wait_recv()
        best = jnp.maximum(best, best_in[step - 1])
    best_ref[...] = best
    for group in range(groups):
        for step in range(1, X):
            x_copy(group, step).wait_send()
        for step in range(1, Z):
            z_copy(group, step).wait_send()
    for step in range(1, FEAT):
        best_copy(step).wait_send()


def per_device(bin_index, node_ids, gradients, hessians):
    feature_count, row_count = bin_index.shape
    groups = feature_count // GROUP
    vmem = pl.BlockSpec(memory_space=pltpu.VMEM)
    dma = pltpu.SemaphoreType.DMA
    gains, best = pl.pallas_call(
        kernel,
        out_shape=(
            jax.ShapeDtypeStruct((1, feature_count, BINS), f32),
            jax.ShapeDtypeStruct((8, LANES), f32),
        ),
        in_specs=[vmem] * 4,
        out_specs=(vmem, vmem),
        scratch_shapes=[
            pltpu.VMEM((LANES, row_count), bf16),
            pltpu.VMEM((2, GROUP * HALF, LANES), f32),
            pltpu.VMEM((groups, X, GROUP, 2 * Z, BINS), f32),
            pltpu.VMEM((groups, X - 1, GROUP, 2 * Z, BINS), f32),
            pltpu.VMEM((groups, Z, 2 * GROUP, BINS), f32),
            pltpu.VMEM((groups, Z - 1, 2 * GROUP, BINS), f32),
            pltpu.VMEM((8, LANES), f32),
            pltpu.VMEM((FEAT - 1, 8, LANES), f32),
            dma((groups, X - 1)),
            dma((groups, X - 1)),
            dma((groups, Z - 1)),
            dma((groups, Z - 1)),
            dma((FEAT - 1,)),
            dma((FEAT - 1,)),
        ],
        compiler_params=pltpu.CompilerParams(
            collective_id=0, has_side_effects=True, vmem_limit_bytes=48 * 2**20
        ),
    )(
        bin_index,
        node_ids.reshape(1, row_count),
        gradients.reshape(1, row_count),
        hessians.reshape(1, row_count),
    )
    return gains, best[0, :1]


def solution(mesh):
    in_specs = (P("feat", "rows"), P("rows"), P("rows"), P("rows"))
    out_specs = (P("rows", "feat", None), P("rows"))
    return jax.shard_map(
        per_device, mesh=mesh, in_specs=in_specs, out_specs=out_specs, check_vma=False
    )
```

time: 99.4 us -> 42.7 us (0.43)
  blocking collectives: 49.5 us -> 0 us
  Pallas kernels: 0 us -> 37.3 us
  matrix products: 29.7 us -> 0 us
  local copies, waits for them, and re-layouts: 11.4 us -> 4.42 us
  other arithmetic: 5.42 us -> 0 us
  loops' own time: 1.82 us -> 0 us
    all_to_all x2 -> x0, blocking collectives: 49.5 us -> none  [the longest x1 37.9 us: sum_at_owner(): lax.all_to_all(tiles, axis, split_axis=0, concat_axis=0, tiled=True)]
    pallas_call x0 -> x1, Pallas kernels: none -> 37.3 us  [per_device(): pl.pallas_call(kernel, out_shape=(jax.ShapeDtypeStruct((1, feature_count,...]
    dot_general x32 -> x0, matrix products: 29.7 us -> none  [accumulate(): lax.dot_general(weighted, bin_hot, (((0,), (0,)), ((), ())), preferred_el...]
    slice x4 -> x1, local copies, waits for them, and re-layouts: 5.69 us -> 0.51 us  [per_device(): return (gains, best[0, :1])]
    unnamed x16 -> x9, local copies, waits for them, and re-layouts: 0.89 us -> 3.91 us
    dynamic_slice x6 -> x0, local copies, waits for them, and re-layouts: 2.63 us -> none  [the longest x2 1.45 us: accumulate(): nodes_here = lax.dynamic_slice_in_dim(node_ids, offset, row_block, 0)]
    convert_element_type x5 -> x0, other arithmetic: 2.01 us -> none  [the longest x2 1.1 us: accumulate(): weighted = (node_hot[:, :, None] * values_here[:, None, :]).astype(jnp.bf...]
    another operation x1 -> x0, loops' own time: 1.82 us -> none  [per_device(): lax.scan(accumulate, start_sums, jnp.arange(block_count, dtype=jnp.int32))]
where the time goes in v1:
time: 42.7 us; the launch traced here: 42.4 us
  Pallas kernels  37.3 us (87%)
  local copies, waits for them, and re-layouts  4.42 us (10%)
  between operations  0.65 us (2%)
    pallas_call x1, Pallas kernels, per_device(): pl.pallas_call(kernel, out_shape=(jax.ShapeDtypeStruct((1, feature_count,...  37.3 us
    unnamed x9, local copies, waits for them, and re-layouts  3.91 us

profile of v1, /device:TPU:1, one launch (start us, length us, event | category | flops | bytes accessed | tf_op | source)
XLA Modules:
  0.0 42.4 jit_solution(6715661461911211580)
XLA Ops:
  0.6 0.0 copy-start
  0.6 1.0 %copy-done = s32[16,8192]{1,0:T(8,128)S(1)} copy-done((s32[16,8192]{1,0:T(8,128)S(1)}, s32[16,8192]{1,0:T(8,128)}, u32[]{:S(2)}) %copy-start) | copy-done | bytes 524312
  1.7 0.0 copy-start.1
  1.7 0.8 %copy-done.1 = s32[8192]{0:T(1024)S(1)} copy-done((s32[8192]{0:T(1024)S(1)}, s32[8192]{0:T(1024)}, u32[]{:S(2)}) %copy-start.1) | copy-done | bytes 32792
  2.4 0.0 copy-start.2
  2.4 0.8 %copy-done.2 = s32[8192]{0:T(1024)S(1)} copy-done((s32[8192]{0:T(1024)S(1)}, s32[8192]{0:T(1024)}, u32[]{:S(2)}) %copy-start.2) | copy-done | bytes 32792
  3.2 0.0 copy-start.3
  3.2 0.8 %copy-done.3 = s32[8192]{0:T(1024)S(1)} copy-done((s32[8192]{0:T(1024)S(1)}, s32[8192]{0:T(1024)}, u32[]{:S(2)}) %copy-start.3) | copy-done | bytes 32792
  3.9 37.3 %shard_map.59 = (f32[1,16,256]{2,1,0:T(8,128)S(1)}, f32[8,128]{1,0:T(8,128)S(1)}) custom-call(s32[16,8192]{1,0:T(8,128)S(1)} %copy-done, s32[1,8192]{1,0:T(1,128)S(1)} %bitcast.4, s32[1,8192]{1,0:T(1,128)S(1)} %bitcast.5, s32[1,8192]{1,0:T(1,128)S(1)} %bitcast.6), custom_call_target="tpu_custom_call" | custom-call | tf_op jit(solution)/shard_map/pallas_call | solution.py:254
  41.3 0.5 %slice.3 = f32[1,1]{1,0:T(1,128)} slice(f32[8,128]{1,0:T(8,128)S(1)} %get-tuple-element.5), slice={[0:1], [0:1]} | slice | bytes 8 | tf_op jit(solution)/shard_map/slice | solution.py:287
  41.8 0.6 %copy.7 = f32[1,16,256]{2,1,0:T(8,128)} copy(f32[1,16,256]{2,1,0:T(8,128)S(1)} %get-tuple-element.8) | data formatting | bytes 32768
Async XLA Ops:
  0.6 1.0 %copy-start = (s32[16,8192]{1,0:T(8,128)S(1)}, s32[16,8192]{1,0:T(8,128)}, u32[]{:S(2)}) copy-start(s32[16,8192]{1,0:T(8,128)} %bins_ref.1) | copy-start | bytes 1572868
  1.7 0.8 %copy-start.1 = (s32[8192]{0:T(1024)S(1)}, s32[8192]{0:T(1024)}, u32[]{:S(2)}) copy-start(s32[8192]{0:T(1024)} %param.5) | copy-start | bytes 98308
  2.4 0.8 %copy-start.2 = (s32[8192]{0:T(1024)S(1)}, s32[8192]{0:T(1024)}, u32[]{:S(2)}) copy-start(s32[8192]{0:T(1024)} %param.6) | copy-start | bytes 98308
  3.2 0.8 %copy-start.3 = (s32[8192]{0:T(1024)S(1)}, s32[8192]{0:T(1024)}, u32[]{:S(2)}) copy-start(s32[8192]{0:T(1024)} %param.7) | copy-start | bytes 98308

commit v2 on v1

v2 whole, which is shorter than its diff:
```python
import functools

import jax
import jax.numpy as jnp
from jax import lax
from jax.experimental import pallas as pl
from jax.experimental.pallas import tpu as pltpu
from jax.sharding import PartitionSpec as P

BINS = 256
HALF = 128
LANES = 128
BASE = 9
TOP = 8192
X = 4
Z = 8
FEAT = 8
GROUPS = (4, 4, 4, 2, 2)
RELAYED = 4
LAGS = (4, 8, 14)
BLOCK = 512
UNROLL = 16
shrinkage = 1.0
MESH = pl.DeviceIdType.MESH
f32 = jnp.float32
bf16 = jnp.bfloat16


def rows_of(row):
    return jnp.broadcast_to(row, (16, LANES)).astype(f32).astype(bf16)


def digit_rows(grad, hess):
    grad8 = jnp.broadcast_to(grad, (8, LANES))
    hess8 = jnp.broadcast_to(hess, (8, LANES))
    return jnp.concatenate([grad8, hess8], 0).astype(bf16)


def weights_of(node_ref, grad_ref, hess_ref, start, nodes_at):
    columns = []
    for tile in range(BLOCK // LANES):
        here = pl.ds(start + tile * LANES, LANES)
        node = rows_of(node_ref[0:1, here])
        grad = grad_ref[0:1, here].astype(f32)
        hess = hess_ref[0:1, here].astype(f32)
        grad_high = jnp.round(grad * (1.0 / BASE))
        hess_high = jnp.round(hess * (1.0 / BASE))
        low = digit_rows(grad - BASE * grad_high, hess - BASE * hess_high)
        high = digit_rows(grad_high, hess_high)
        none = jnp.zeros_like(low)
        masks = [node == nodes for nodes in nodes_at]
        column = [jnp.where(mask, low, none) for mask in masks]
        column += [jnp.where(mask, high, none) for mask in masks]
        columns.append(jnp.concatenate(column, 0))
    return jnp.concatenate(columns, 1)


def kernel(*refs):
    groups = len(GROUPS)
    take = iter(refs)
    some = lambda count: [next(take) for unused in range(count)]
    bins_hbm, node_hbm, grad_hbm, hess_hbm, out_ref, best_ref = some(6)
    bins_ref, node_ref, grad_ref, hess_ref, weights, total = some(6)
    partial, x_in, z_out, z_in = some(groups), some(groups), some(groups), some(groups)
    relay_in, relay_out = some(RELAYED), some(RELAYED)
    best_out, best_in, load_sem = some(3)
    x_send, x_recv, r_send, r_recv, z_send, z_recv, b_send, b_recv = some(8)

    feature_count, row_count = bins_ref.shape
    feat = lax.axis_index("feat")
    rows = lax.axis_index("rows")
    my_z = rows // X
    my_x = rows % X

    loads = [
        pltpu.make_async_copy(source, target, load_sem.at[number])
        for number, (source, target) in enumerate(
            [
                (node_hbm, node_ref),
                (grad_hbm, grad_ref),
                (hess_hbm, hess_ref),
                (bins_hbm.at[0:8], bins_ref.at[0:8]),
                (bins_hbm.at[8:16], bins_ref.at[8:16]),
            ]
        )
    ]
    for load in loads:
        load.start()

    def device_at(z, x):
        return ((my_z + z) % Z) * X + (my_x + x) % X

    barrier = pltpu.get_barrier_semaphore()
    for step in range(1, X):
        pl.semaphore_signal(
            barrier, inc=1, device_id=(feat, device_at(0, step)), device_id_type=MESH
        )
    for step in range(1, Z):
        pl.semaphore_signal(
            barrier, inc=1, device_id=(feat, device_at(step, 0)), device_id_type=MESH
        )
    for step in range(1, FEAT):
        pl.semaphore_signal(
            barrier, inc=1, device_id=((feat + step) % FEAT, rows), device_id_type=MESH
        )

    bin_at = lax.broadcasted_iota(jnp.int32, (HALF, LANES), 0).astype(f32).astype(bf16)
    nodes_at = [
        ((lax.broadcasted_iota(jnp.int32, (16, LANES), 0) % Z) * X + x).astype(f32).astype(bf16)
        for x in range(X)
    ]
    big = f32(1.5 * 2.0**36)

    def compute(group):
        size_here = GROUPS[group]
        base = sum(GROUPS[:group])
        totals = slice(0, size_here * HALF)

        def block(number, carry):
            start = pl.multiple_of(number * BLOCK, BLOCK)
            row_list = []
            for feature in range(size_here):
                at = base + feature
                columns = []
                for tile in range(BLOCK // LANES):
                    row = bins_ref[at : at + 1, pl.ds(start + tile * LANES, LANES)]
                    upper = row >= HALF
                    low = jnp.where(upper, row - HALF, row)
                    size = jnp.where(upper, TOP, 1)
                    low = jnp.concatenate([rows_of(low)] * (HALF // 16), 0)
                    size = jnp.concatenate([rows_of(size)] * (HALF // 16), 0)
                    columns.append(jnp.where(low <= bin_at, size, jnp.zeros_like(size)))
                row_list.append(jnp.concatenate(columns, 1))
            hot = jnp.concatenate(row_list, 0)
            if group == 0:
                weight = weights_of(node_ref, grad_ref, hess_ref, start, nodes_at)
                weights[:, pl.ds(start, BLOCK)] = weight
            else:
                weight = weights[:, pl.ds(start, BLOCK)]
            product = lax.dot_general(
                hot, weight, (((1,), (1,)), ((), ())), preferred_element_type=f32
            )
            upper_part = (product + big) - big
            total[0, totals, :] += product - upper_part
            total[1, totals, :] += upper_part
            return carry

        total[:, totals, :] = jnp.zeros((2, size_here * HALF, LANES), f32)
        lax.fori_loop(0, row_count // BLOCK, block, 0, unroll=UNROLL)
        count = 4 * size_here
        for feature in range(size_here):
            at = slice(feature * HALF, (feature + 1) * HALF)
            for half in range(2):
                turned = total[half, at, :].T
                joined = turned[: LANES // 2] + BASE * turned[LANES // 2 :]
                if half:
                    joined = joined * (1.0 / TOP)
                for x in range(X):
                    for part in range(2):
                        line = (half * 2 + part) * size_here + feature
                        from_row = x * 2 * Z + part * Z
                        partial[group][pl.ds(x * Z * count + line, Z, stride=count), :] = joined[
                            from_row : from_row + Z
                        ]

    def lines_for(group, step):
        lines = 4 * GROUPS[group] * Z
        return pl.multiple_of(((my_x + step) % X) * lines, lines), lines

    def send(source, target, send_sem, recv_sem, device):
        return pltpu.make_async_remote_copy(
            src_ref=source,
            dst_ref=target,
            send_sem=send_sem,
            recv_sem=recv_sem,
            device_id=(feat, device),
            device_id_type=MESH,
        )

    def x_copy(group, step):
        start, lines = lines_for(group, step)
        return send(
            partial[group].at[pl.ds(start, lines)],
            x_in[group].at[step - 1],
            x_send.at[group, step - 1],
            x_recv.at[group, step - 1],
            device_at(0, step),
        )

    def far_copy(group, way):
        start, lines = lines_for(group, 2)
        half = lines // 2
        return send(
            partial[group].at[pl.ds(start + way * half, half)],
            relay_in[group].at[way],
            r_send.at[group, way],
            r_recv.at[group, way],
            device_at(0, 1 - 2 * way),
        )

    def plain_copy(group, way):
        start, lines = lines_for(group, 1 - 2 * way)
        half = lines // 2
        return send(
            partial[group].at[pl.ds(start + (1 - way) * half, half)],
            x_in[group].at[way, pl.ds((1 - way) * half, half)],
            x_send.at[group, way],
            x_recv.at[group, way],
            device_at(0, 1 - 2 * way),
        )

    def added_copy(group, way):
        half = 4 * GROUPS[group] * Z // 2
        return send(
            relay_out[group].at[way],
            x_in[group].at[way, pl.ds(way * half, half)],
            r_send.at[group, 2 + way],
            r_recv.at[group, 2 + way],
            device_at(0, 1 - 2 * way),
        )

    def z_copy(group, step):
        lines = 4 * GROUPS[group]
        source = pl.multiple_of(((my_z + step) % Z) * lines, lines)
        return pltpu.make_async_remote_copy(
            src_ref=z_out[group].at[pl.ds(source, lines)],
            dst_ref=z_in[group].at[step - 1],
            send_sem=z_send.at[group, step - 1],
            recv_sem=z_recv.at[group, step - 1],
            device_id=(feat, device_at(step, 0)),
            device_id_type=MESH,
        )

    def best_copy(step):
        return pltpu.make_async_remote_copy(
            src_ref=best_out,
            dst_ref=best_in.at[step - 1],
            send_sem=b_send.at[step - 1],
            recv_sem=b_recv.at[step - 1],
            device_id=((feat + step) % FEAT, rows),
            device_id_type=MESH,
        )

    def start_x(group):
        if group < RELAYED:
            for way in range(2):
                far_copy(group, way).start()
            for way in range(2):
                plain_copy(group, way).start()
        else:
            for step in (2, 1, 3):
                x_copy(group, step).start()

    def relay(group):
        for way in range(2):
            far_copy(group, way).wait_recv()
            start, lines = lines_for(group, 1 - 2 * way)
            half = lines // 2
            mine = partial[group][pl.ds(start + way * half, half), :]
            relay_out[group][way] = relay_in[group][way] + mine
            added_copy(group, way).start()

    def x_to_z(group):
        start, lines = lines_for(group, 0)
        summed = partial[group][pl.ds(start, lines), :]
        if group < RELAYED:
            for way in range(2):
                plain_copy(group, way).wait_recv()
                added_copy(group, way).wait_recv()
                summed = summed + x_in[group][way]
        else:
            for step in range(1, X):
                x_copy(group, step).wait_recv()
                summed = summed + x_in[group][step - 1]
        z_out[group][...] = summed
        for step in (4, 3, 5, 2, 6, 1, 7):
            z_copy(group, step).start()

    def gains_at(group, summed):
        size = GROUPS[group]
        base = sum(GROUPS[:group])
        first = summed[: 2 * size]
        second = summed[2 * size :] + first[:, HALF - 1 :]
        whole = second[:, HALF - 1 :]
        whole_grad, whole_hess = whole[:size], whole[size:]
        unsplit = whole_grad * whole_grad / (whole_hess + shrinkage)
        for half, left in enumerate((first, second)):
            right = whole - left
            left_grad, left_hess = left[:size], left[size:]
            right_grad, right_hess = right[:size], right[size:]
            out_ref[0, base : base + size, half * HALF : (half + 1) * HALF] = 0.5 * (
                left_grad * left_grad / (left_hess + shrinkage)
                + right_grad * right_grad / (right_hess + shrinkage)
                - unsplit
            )

    def finish(group):
        for step in range(1, Z):
            z_copy(group, step).wait_recv()
        lines = 4 * GROUPS[group]
        summed = z_out[group][pl.ds(pl.multiple_of(my_z * lines, lines), lines), :]
        for step in range(1, Z):
            summed = summed + z_in[group][step - 1]
        gains_at(group, summed)

    for number in range(4):
        loads[number].wait()
    events = []
    done = 0
    for group in range(groups):
        done += GROUPS[group]
        relayed = group < RELAYED
        if relayed:
            events.append((done + LAGS[0], 0, group, relay))
        events.append((done + LAGS[relayed], 1, group, x_to_z))
        events.append((done + LAGS[relayed] + LAGS[2] - LAGS[1], 2, group, finish))
    events.sort(key=lambda event: event[:3])
    done = 0
    for group in range(groups):
        compute(group)
        done += GROUPS[group]
        if group == 0:
            loads[4].wait()
            pl.semaphore_wait(barrier, X - 1 + Z - 1 + FEAT - 1)
        start_x(group)
        while events and (events[0][0] <= done or group == groups - 1):
            unused_time, unused_stage, which, action = events.pop(0)
            action(which)
    gains = out_ref[0]
    top = jnp.max(jnp.max(gains, axis=1, keepdims=True), axis=0, keepdims=True)
    best_out[...] = jnp.broadcast_to(top, best_out.shape)
    for step in range(1, FEAT):
        best_copy(step).start()
    for group in range(groups):
        if group < RELAYED:
            for way in range(2):
                far_copy(group, way).wait_send()
                plain_copy(group, way).wait_send()
                added_copy(group, way).wait_send()
        else:
            for step in range(1, X):
                x_copy(group, step).wait_send()
        for step in range(1, Z):
            z_copy(group, step).wait_send()
    best = best_out[...]
    for step in range(1, FEAT):
        best_copy(step).wait_recv()
        best = jnp.maximum(best, best_in[step - 1])
    best_ref[...] = best
    for step in range(1, FEAT):
        best_copy(step).wait_send()


def per_device(bin_index, node_ids, gradients, hessians):
    feature_count, row_count = bin_index.shape
    groups = len(GROUPS)
    vmem = pl.BlockSpec(memory_space=pltpu.VMEM)
    hbm = pl.BlockSpec(memory_space=pltpu.HBM)
    dma = pltpu.SemaphoreType.DMA
    table = lambda *shape: pltpu.VMEM((*shape, LANES), f32)
    gains, best = pl.pallas_call(
        kernel,
        out_shape=(
            jax.ShapeDtypeStruct((1, feature_count, BINS), f32),
            jax.ShapeDtypeStruct((8, LANES), f32),
        ),
        in_specs=[hbm] * 4,
        out_specs=(vmem, vmem),
        scratch_shapes=[
            pltpu.VMEM((feature_count, row_count), jnp.int32),
            *[pltpu.VMEM((1, row_count), jnp.int32)] * 3,
            pltpu.VMEM((LANES, row_count), bf16),
            table(2, max(GROUPS) * HALF),
            *[table(X * Z * 4 * size) for size in GROUPS],
            *[table(X - 1, Z * 4 * size) for size in GROUPS],
            *[table(Z * 4 * size) for size in GROUPS],
            *[table(Z - 1, 4 * size) for size in GROUPS],
            *[table(2, Z * 2 * size) for size in GROUPS[:RELAYED]] * 2,
            table(8),
            table(FEAT - 1, 8),
            dma((5,)),
            dma((groups, X - 1)),
            dma((groups, X - 1)),
            dma((groups, 4)),
            dma((groups, 4)),
            dma((groups, Z - 1)),
            dma((groups, Z - 1)),
            dma((FEAT - 1,)),
            dma((FEAT - 1,)),
        ],
        compiler_params=pltpu.CompilerParams(
            collective_id=0, has_side_effects=True, vmem_limit_bytes=55200 * 1024
        ),
    )(
        bin_index,
        node_ids.reshape(1, row_count),
        gradients.reshape(1, row_count),
        hessians.reshape(1, row_count),
    )
    return gains, best[0, :1]


def solution(mesh):
    in_specs = (P("feat", "rows"), P("rows"), P("rows"), P("rows"))
    out_specs = (P("rows", "feat", None), P("rows"))
    return jax.shard_map(
        per_device, mesh=mesh, in_specs=in_specs, out_specs=out_specs, check_vma=False
    )
```

time: 42.7 us -> 37.3 us (0.87)
  local copies, waits for them, and re-layouts: 4.42 us -> 1.12 us
  Pallas kernels: 37.3 us -> 35.5 us
    unnamed x9 -> x1, local copies, waits for them, and re-layouts: 3.91 us -> 0.6 us
    pallas_call x1, Pallas kernels: 37.3 us -> 35.5 us  [per_device(): pl.pallas_call(kernel, out_shape=(jax.ShapeDtypeStruct((1, feature_count,...]
where the time goes in v2:
time: 37.3 us; the launch traced here: 37.2 us
  Pallas kernels  35.5 us (95%)
  local copies, waits for them, and re-layouts  1.12 us (3%)
  between operations  0.64 us (2%)
    pallas_call x1, Pallas kernels, per_device(): pl.pallas_call(kernel, out_shape=(jax.ShapeDtypeStruct((1, feature_count,...  35.5 us

profile of v2, /device:TPU:1, one launch (start us, length us, event | category | flops | bytes accessed | tf_op | source)
XLA Modules:
  0.0 37.2 jit_solution(16452710611675493767)
XLA Ops:
  0.6 35.5 %shard_map.59 = (f32[1,16,256]{2,1,0:T(8,128)S(1)}, f32[8,128]{1,0:T(8,128)S(1)}) custom-call(s32[16,8192]{1,0:T(8,128)} %refs_0_.1, s32[1,8192]{1,0:T(1,128)} %bitcast.4, s32[1,8192]{1,0:T(1,128)} %bitcast.5, s32[1,8192]{1,0:T(1,128)} %bitcast.6), custom_call_target="tpu_custom_call" | custom-call | tf_op jit(solution)/shard_map/pallas_call | solution.py:361
  36.1 0.5 %slice.3 = f32[1,1]{1,0:T(1,128)} slice(f32[8,128]{1,0:T(8,128)S(1)} %get-tuple-element.5), slice={[0:1], [0:1]} | slice | bytes 8 | tf_op jit(solution)/shard_map/slice | solution.py:400
  36.6 0.6 %copy.7 = f32[1,16,256]{2,1,0:T(8,128)} copy(f32[1,16,256]{2,1,0:T(8,128)S(1)} %get-tuple-element.8) | data formatting | bytes 32768

commit v3 on v2

--- a/solution.py
+++ b/solution.py
@@ -15,9 +15,9 @@
 X = 4
 Z = 8
 FEAT = 8
-GROUPS = (4, 4, 4, 2, 2)
-RELAYED = 4
-LAGS = (4, 8, 14)
+GROUPS = (5, 5, 4, 2)
+MODES = "rzdd"
+LAGS = (4, 9, 20)
 BLOCK = 512
 UNROLL = 16
 shrinkage = 1.0
@@ -62,7 +62,7 @@
     bins_hbm, node_hbm, grad_hbm, hess_hbm, out_ref, best_ref = some(6)
     bins_ref, node_ref, grad_ref, hess_ref, weights, total = some(6)
     partial, x_in, z_out, z_in = some(groups), some(groups), some(groups), some(groups)
-    relay_in, relay_out = some(RELAYED), some(RELAYED)
+    relay_in, relay_out = some(groups), some(groups)
     best_out, best_in, load_sem = some(3)
     x_send, x_recv, r_send, r_recv, z_send, z_recv, b_send, b_recv = some(8)
 
@@ -159,9 +159,11 @@
                     for part in range(2):
                         line = (half * 2 + part) * size_here + feature
                         from_row = x * 2 * Z + part * Z
-                        partial[group][pl.ds(x * Z * count + line, Z, stride=count), :] = joined[
-                            from_row : from_row + Z
-                        ]
+                        if MODES[group] == "z":
+                            lines = pl.ds(x * count + line, Z, stride=X * count)
+                        else:
+                            lines = pl.ds(x * Z * count + line, Z, stride=count)
+                        partial[group][lines, :] = joined[from_row : from_row + Z]
 
     def lines_for(group, step):
         lines = 4 * GROUPS[group] * Z
@@ -231,6 +233,28 @@
             device_id_type=MESH,
         )
 
+    def z_first_copy(group, step):
+        lines = 4 * GROUPS[group] * X
+        start = pl.multiple_of(((my_z + step) % Z) * lines, lines)
+        return send(
+            partial[group].at[pl.ds(start, lines)],
+            x_in[group].at[step - 1],
+            x_send.at[group, step - 1],
+            x_recv.at[group, step - 1],
+            device_at(step, 0),
+        )
+
+    def x_last_copy(group, step):
+        lines = 4 * GROUPS[group]
+        start = pl.multiple_of(((my_x + step) % X) * lines, lines)
+        return send(
+            z_out[group].at[pl.ds(start, lines)],
+            z_in[group].at[step - 1],
+            z_send.at[group, step - 1],
+            z_recv.at[group, step - 1],
+            device_at(0, step),
+        )
+
     def best_copy(step):
         return pltpu.make_async_remote_copy(
             src_ref=best_out,
@@ -242,11 +266,14 @@
         )
 
     def start_x(group):
-        if group < RELAYED:
+        if MODES[group] == "r":
             for way in range(2):
                 far_copy(group, way).start()
             for way in range(2):
                 plain_copy(group, way).start()
+        elif MODES[group] == "z":
+            for step in (4, 3, 5, 2, 6, 1, 7):
+                z_first_copy(group, step).start()
         else:
             for step in (2, 1, 3):
                 x_copy(group, step).start()
@@ -260,10 +287,22 @@
             relay_out[group][way] = relay_in[group][way] + mine
             added_copy(group, way).start()
 
+    def z_to_x(group):
+        lines = 4 * GROUPS[group] * X
+        summed = partial[group][pl.ds(pl.multiple_of(my_z * lines, lines), lines), :]
+        for step in range(1, Z):
+            z_first_copy(group, step).wait_recv()
+            summed = summed + x_in[group][step - 1]
+        z_out[group][...] = summed
+        for step in (2, 1, 3):
+            x_last_copy(group, step).start()
+
     def x_to_z(group):
+        if MODES[group] == "z":
+            return z_to_x(group)
         start, lines = lines_for(group, 0)
         summed = partial[group][pl.ds(start, lines), :]
-        if group < RELAYED:
+        if MODES[group] == "r":
             for way in range(2):
                 plain_copy(group, way).wait_recv()
                 added_copy(group, way).wait_recv()
@@ -295,6 +334,13 @@
             )
 
     def finish(group):
+        if MODES[group] == "z":
+            lines = 4 * GROUPS[group]
+            summed = z_out[group][pl.ds(pl.multiple_of(my_x * lines, lines), lines), :]
+            for step in range(1, X):
+                x_last_copy(group, step).wait_recv()
+                summed = summed + z_in[group][step - 1]
+            return gains_at(group, summed)
         for step in range(1, Z):
             z_copy(group, step).wait_recv()
         lines = 4 * GROUPS[group]
@@ -309,8 +355,8 @@
     done = 0
     for group in range(groups):
         done += GROUPS[group]
-        relayed = group < RELAYED
-        if relayed:
+        relayed = MODES[group] != "d"
+        if MODES[group] == "r":
             events.append((done + LAGS[0], 0, group, relay))
         events.append((done + LAGS[relayed], 1, group, x_to_z))
         events.append((done + LAGS[relayed] + LAGS[2] - LAGS[1], 2, group, finish))
@@ -332,16 +378,22 @@
     for step in range(1, FEAT):
         best_copy(step).start()
     for group in range(groups):
-        if group < RELAYED:
+        if MODES[group] == "r":
             for way in range(2):
                 far_copy(group, way).wait_send()
                 plain_copy(group, way).wait_send()
                 added_copy(group, way).wait_send()
-        else:
+        elif MODES[group] == "d":
             for step in range(1, X):
                 x_copy(group, step).wait_send()
-        for step in range(1, Z):
-            z_copy(group, step).wait_send()
+        if MODES[group] == "z":
+            for step in range(1, Z):
+                z_first_copy(group, step).wait_send()
+            for step in range(1, X):
+                x_last_copy(group, step).wait_send()
+        else:
+            for step in range(1, Z):
+                z_copy(group, step).wait_send()
     best = best_out[...]
     for step in range(1, FEAT):
         best_copy(step).wait_recv()
@@ -357,6 +409,7 @@
     vmem = pl.BlockSpec(memory_space=pltpu.VMEM)
     hbm = pl.BlockSpec(memory_space=pltpu.HBM)
     dma = pltpu.SemaphoreType.DMA
+    stages = [(size, *((Z, X) if mode == "z" else (X, Z))) for size, mode in zip(GROUPS, MODES)]
     table = lambda *shape: pltpu.VMEM((*shape, LANES), f32)
     gains, best = pl.pallas_call(
         kernel,
@@ -372,15 +425,15 @@
             pltpu.VMEM((LANES, row_count), bf16),
             table(2, max(GROUPS) * HALF),
             *[table(X * Z * 4 * size) for size in GROUPS],
-            *[table(X - 1, Z * 4 * size) for size in GROUPS],
-            *[table(Z * 4 * size) for size in GROUPS],
-            *[table(Z - 1, 4 * size) for size in GROUPS],
-            *[table(2, Z * 2 * size) for size in GROUPS[:RELAYED]] * 2,
+            *[table(first - 1, second * 4 * size) for size, first, second in stages],
+            *[table(second * 4 * size) for size, first, second in stages],
+            *[table(second - 1, 4 * size) for size, first, second in stages],
+            *[table(2, Z * 2 * size) for size in GROUPS] * 2,
             table(8),
             table(FEAT - 1, 8),
             dma((5,)),
-            dma((groups, X - 1)),
-            dma((groups, X - 1)),
+            dma((groups, Z - 1)),
+            dma((groups, Z - 1)),
             dma((groups, 4)),
             dma((groups, 4)),
             dma((groups, Z - 1)),

time: 37.3 us -> 36.1 us (0.968)
  Pallas kernels: 35.5 us -> 34.2 us
    pallas_call x1, Pallas kernels: 35.5 us -> 34.2 us  [per_device(): pl.pallas_call(kernel, out_shape=(jax.ShapeDtypeStruct((1, feature_count,...]
where the time goes in v3:
time: 36.1 us; the launch traced here: 36 us
  Pallas kernels  34.2 us (95%)
  local copies, waits for them, and re-layouts  1.12 us (3%)
  between operations  0.64 us (2%)
    pallas_call x1, Pallas kernels, per_device(): pl.pallas_call(kernel, out_shape=(jax.ShapeDtypeStruct((1, feature_count,...  34.2 us

profile of v3, /device:TPU:1, one launch (start us, length us, event | category | flops | bytes accessed | tf_op | source)
XLA Modules:
  0.0 36.0 jit_solution(12708924526364657634)
XLA Ops:
  0.6 34.2 %shard_map.59 = (f32[1,16,256]{2,1,0:T(8,128)S(1)}, f32[8,128]{1,0:T(8,128)S(1)}) custom-call(s32[16,8192]{1,0:T(8,128)} %refs_0_.1, s32[1,8192]{1,0:T(1,128)} %bitcast.4, s32[1,8192]{1,0:T(1,128)} %bitcast.5, s32[1,8192]{1,0:T(1,128)} %bitcast.6), custom_call_target="tpu_custom_call" | custom-call | tf_op jit(solution)/shard_map/pallas_call | solution.py:414
  34.9 0.5 %slice.3 = f32[1,1]{1,0:T(1,128)} slice(f32[8,128]{1,0:T(8,128)S(1)} %get-tuple-element.5), slice={[0:1], [0:1]} | slice | bytes 8 | tf_op jit(solution)/shard_map/slice | solution.py:453
  35.4 0.6 %copy.7 = f32[1,16,256]{2,1,0:T(8,128)} copy(f32[1,16,256]{2,1,0:T(8,128)S(1)} %get-tuple-element.8) | data formatting | bytes 32768

commit v4 on v3

--- a/solution.py
+++ b/solution.py
@@ -15,7 +15,7 @@
 X = 4
 Z = 8
 FEAT = 8
-GROUPS = (5, 5, 4, 2)
+GROUPS = (7, 4, 3, 2)
 MODES = "rzdd"
 LAGS = (4, 9, 20)
 BLOCK = 512
@@ -375,7 +375,7 @@
     gains = out_ref[0]
     top = jnp.max(jnp.max(gains, axis=1, keepdims=True), axis=0, keepdims=True)
     best_out[...] = jnp.broadcast_to(top, best_out.shape)
-    for step in range(1, FEAT):
+    for step in (4, 5, 3, 2, 6, 7, 1):
         best_copy(step).start()
     for group in range(groups):
         if MODES[group] == "r":
@@ -398,7 +398,7 @@
     for step in range(1, FEAT):
         best_copy(step).wait_recv()
         best = jnp.maximum(best, best_in[step - 1])
-    best_ref[...] = best
+    best_ref[...] = jnp.broadcast_to(best, best_ref.shape)
     for step in range(1, FEAT):
         best_copy(step).wait_send()
 
@@ -429,8 +429,8 @@
             *[table(second * 4 * size) for size, first, second in stages],
             *[table(second - 1, 4 * size) for size, first, second in stages],
             *[table(2, Z * 2 * size) for size in GROUPS] * 2,
-            table(8),
-            table(FEAT - 1, 8),
+            table(1),
+            table(FEAT - 1, 1),
             dma((5,)),
             dma((groups, Z - 1)),
             dma((groups, Z - 1)),

time: 36.1 us -> 35.1 us (0.972)
  Pallas kernels: 34.2 us -> 33.2 us
    pallas_call x1, Pallas kernels: 34.2 us -> 33.2 us  [per_device(): pl.pallas_call(kernel, out_shape=(jax.ShapeDtypeStruct((1, feature_count,...]
where the time goes in v4:
time: 35.1 us; the launch traced here: 35 us
  Pallas kernels  33.2 us (95%)
  local copies, waits for them, and re-layouts  1.12 us (3%)
  between operations  0.64 us (2%)
    pallas_call x1, Pallas kernels, per_device(): pl.pallas_call(kernel, out_shape=(jax.ShapeDtypeStruct((1, feature_count,...  33.2 us

profile of v4, /device:TPU:1, one launch (start us, length us, event | category | flops | bytes accessed | tf_op | source)
XLA Modules:
  0.0 35.0 jit_solution(11310763353206064060)
XLA Ops:
  0.6 33.2 %shard_map.59 = (f32[1,16,256]{2,1,0:T(8,128)S(1)}, f32[8,128]{1,0:T(8,128)S(1)}) custom-call(s32[16,8192]{1,0:T(8,128)} %refs_0_.1, s32[1,8192]{1,0:T(1,128)} %bitcast.4, s32[1,8192]{1,0:T(1,128)} %bitcast.5, s32[1,8192]{1,0:T(1,128)} %bitcast.6), custom_call_target="tpu_custom_call" | custom-call | tf_op jit(solution)/shard_map/pallas_call | solution.py:414
  33.9 0.5 %slice.3 = f32[1,1]{1,0:T(1,128)} slice(f32[8,128]{1,0:T(8,128)S(1)} %get-tuple-element.5), slice={[0:1], [0:1]} | slice | bytes 8 | tf_op jit(solution)/shard_map/slice | solution.py:453
  34.4 0.6 %copy.7 = f32[1,16,256]{2,1,0:T(8,128)} copy(f32[1,16,256]{2,1,0:T(8,128)S(1)} %get-tuple-element.8) | data formatting | bytes 32768
